TPU v7x, 32 devices: a whole 2x2x4 slice. The times are simulated.
32 devices in a mesh: batch: 16 (over z, y, core), rows: 2 (over x).
Axes of the slice: x: 2, y: 2, z: 4, core: 2. Of those that a mesh axis runs over, the one named last changes fastest.
Arguments:
- block_input: bfloat16 [16, 16, 64, 384], P('batch', 'rows'), may hold values from -6 to 6
- output_grad: bfloat16 [16, 16, 64, 768], P('batch', 'rows'), may hold values from -6 to 6
- conv_weight: float32 [384, 1152], P(None, 'batch'), may hold values from -12 to 12
- conv_gain: float32 [384], replicated, may hold values from 0.1 to 1.9
- conv_momentum: float32 [384, 1152], P(None, 'batch'), may hold values from -0.6 to 0.6
- proj_weight: float32 [768, 384], P(None, 'batch'), may hold values from -12 to 12
- proj_gain: float32 [768], replicated, may hold values from 0.1 to 1.9
- proj_momentum: float32 [768, 384], P(None, 'batch'), may hold values from -0.6 to 0.6
Outputs:
- input_grad: bfloat16 [16, 16, 64, 384], P('batch', 'rows')
- new_conv_weight: float32 [384, 1152], P(None, 'batch')
- new_conv_momentum: float32 [384, 1152], P(None, 'batch')
- new_proj_weight: float32 [768, 384], P(None, 'batch')
- new_proj_momentum: float32 [768, 384], P(None, 'batch')
All inputs are finite; a program needn't handle non-finite values.
Results may differ from a plain program's by a relative error of at most 0.0031.
The roundings to bfloat16 on the way count: a program that leaves them out, or rounds other values in their place, can miss the bound.
Values may be sent and summed in bfloat16 or wider, within the bound.
A program may use at most 64 MiB of HBM per device.

v0:
```python
import jax
import jax.numpy as jnp
from jax import lax
from jax.sharding import PartitionSpec as P

CH = 384
GW = 128
OUT = 768


ws_eps = 0.0001
clip_ratio = 0.05
momentum_rate = 0.9
learn_rate = 1.6
norm_eps = 1e-06


def padded(cells, sides, width):
    for axis, dim in sides:
        count = lax.axis_size(axis)
        ends = count - 1
        head = lax.slice_in_dim(cells, 0, width, axis=dim)
        tail = lax.slice_in_dim(cells, cells.shape[dim] - width, cells.shape[dim], axis=dim)
        cells = jnp.concatenate(
            [
                lax.ppermute(tail, axis, [(i, (i + 1) % count) for i in range(ends)]),
                cells,
                lax.ppermute(head, axis, [((i + 1) % count, i) for i in range(ends)]),
            ],
            axis=dim,
        )
    return cells


def gelu_slope(values):
    return jax.jvp(jax.nn.gelu, (values,), (jnp.ones_like(values),))[1]


def raw_gradient(grad_std, centered, gain_row, factor, grad_sum, grad_proj, fan_in):
    coef_one = gain_row * factor
    coef_two = gain_row * factor**3 * grad_proj
    return (
        coef_one[:, None] * (grad_std - (grad_sum / fan_in)[:, None]) - coef_two[:, None] * centered
    )


def apply_update(weight, momentum, raw_grad, weight_sq, grad_sq):
    clip_scale = jnp.minimum(1.0, clip_ratio * jnp.sqrt(weight_sq) * lax.rsqrt(grad_sq + norm_eps))
    clipped = raw_grad * clip_scale[:, None]
    new_momentum = momentum_rate * momentum + clipped
    return (weight - learn_rate * (clipped + momentum_rate * new_momentum), new_momentum)


def local(
    block_input,
    output_grad,
    conv_weight,
    conv_gain,
    conv_momentum,
    proj_weight,
    proj_gain,
    proj_momentum,
):
    groups = CH // GW
    conv_fan = 9 * GW
    proj_fan = CH
    totals = lax.psum(
        (
            jnp.sum(conv_weight, axis=1),
            jnp.sum(conv_weight * conv_weight, axis=1),
            jnp.sum(proj_weight, axis=1),
            jnp.sum(proj_weight * proj_weight, axis=1),
        ),
        "batch",
    )
    conv_cent = conv_weight - (totals[0] / conv_fan)[:, None]
    proj_cent = proj_weight - (totals[2] / proj_fan)[:, None]
    spreads = lax.psum(
        (jnp.sum(conv_cent * conv_cent, axis=1), jnp.sum(proj_cent * proj_cent, axis=1)), "batch"
    )
    conv_factor = lax.rsqrt(spreads[0] + ws_eps)
    proj_factor = lax.rsqrt(spreads[1] + ws_eps)
    conv_std = ((conv_gain * conv_factor)[:, None] * conv_cent).astype(jnp.bfloat16)
    proj_std = ((proj_gain * proj_factor)[:, None] * proj_cent).astype(jnp.bfloat16)
    conv_full, proj_full = (
        lax.all_gather(conv_std, "batch", axis=1, tiled=True),
        lax.all_gather(proj_std, "batch", axis=1, tiled=True),
    )
    kernel = conv_full.reshape(groups, GW, 9, GW)
    map_rows = block_input.shape[1]
    map_cols = block_input.shape[2]
    pixels = map_rows * map_cols
    activated = jax.nn.gelu(block_input.astype(jnp.float32)).astype(jnp.bfloat16)
    act_pad = padded(activated, (("rows", 1),), 1)
    act_pad = jnp.pad(act_pad, ((0, 0), (0, 0), (1, 1), (0, 0)))
    patch_list = []
    pre_act = jnp.zeros((pixels, groups, GW), jnp.float32)
    for position in range(9):
        top = position // 3
        left = position % 3
        patch = act_pad[0, top : top + map_rows, left : left + map_cols].reshape(pixels, groups, GW)
        patch_list.append(patch)
        pre_act = pre_act + jnp.einsum(
            "pgi,goi->pgo", patch, kernel[:, :, position, :], preferred_element_type=jnp.float32
        )
    pre_flat = pre_act.reshape(pixels, CH)
    hidden = jax.nn.gelu(pre_flat).astype(jnp.bfloat16)
    upstream = output_grad.reshape(pixels, OUT)
    hidden_grad = jnp.dot(upstream, proj_full, preferred_element_type=jnp.float32)
    pre_grad = (hidden_grad * gelu_slope(pre_flat)).astype(jnp.bfloat16)
    proj_part = jnp.einsum("po,pi->oi", upstream, hidden, preferred_element_type=jnp.float32)
    grad_groups = pre_grad.reshape(pixels, groups, GW)
    conv_terms = jnp.stack(
        [
            jnp.einsum("pgi,pgo->goi", patch, grad_groups, preferred_element_type=jnp.float32)
            for patch in patch_list
        ],
        axis=2,
    )
    conv_part = conv_terms.reshape(CH, 9 * GW)
    grad_pad = padded(pre_grad.reshape(1, map_rows, map_cols, CH), (("rows", 1),), 1)
    grad_pad = jnp.pad(grad_pad, ((0, 0), (0, 0), (1, 1), (0, 0)))
    act_grad = jnp.zeros((pixels, groups, GW), jnp.float32)
    for position in range(9):
        top = 2 - position // 3
        left = 2 - position % 3
        piece = grad_pad[0, top : top + map_rows, left : left + map_cols].reshape(
            pixels, groups, GW
        )
        act_grad = act_grad + jnp.einsum(
            "pgo,goi->pgi", piece, kernel[:, :, position, :], preferred_element_type=jnp.float32
        )
    slope = gelu_slope(block_input.astype(jnp.float32))
    input_grad = (act_grad.reshape(block_input.shape) * slope).astype(jnp.bfloat16)
    shares = (
        lax.psum_scatter(conv_part, "batch", scatter_dimension=1, tiled=True),
        lax.psum_scatter(proj_part, "batch", scatter_dimension=1, tiled=True),
    )
    conv_grad, proj_grad = lax.psum((shares[0], shares[1]), "rows")
    images = lax.axis_size("batch")
    conv_grad = conv_grad / images
    proj_grad = proj_grad / images
    conv_sum = jnp.sum(conv_grad, axis=1)
    conv_proj = jnp.sum(conv_grad * conv_cent, axis=1)
    proj_sum = jnp.sum(proj_grad, axis=1)
    proj_proj = jnp.sum(proj_grad * proj_cent, axis=1)
    row_totals = lax.psum((conv_sum, conv_proj, proj_sum, proj_proj), "batch")
    conv_raw = raw_gradient(
        conv_grad, conv_cent, conv_gain, conv_factor, row_totals[0], row_totals[1], conv_fan
    )
    proj_raw = raw_gradient(
        proj_grad, proj_cent, proj_gain, proj_factor, row_totals[2], row_totals[3], proj_fan
    )
    squares = lax.psum(
        (jnp.sum(conv_raw * conv_raw, axis=1), jnp.sum(proj_raw * proj_raw, axis=1)), "batch"
    )
    conv_sq = squares[0]
    proj_sq = squares[1]
    new_conv_weight, new_conv_momentum = apply_update(
        conv_weight, conv_momentum, conv_raw, totals[1], conv_sq
    )
    new_proj_weight, new_proj_momentum = apply_update(
        proj_weight, proj_momentum, proj_raw, totals[3], proj_sq
    )
    return (input_grad, new_conv_weight, new_conv_momentum, new_proj_weight, new_proj_momentum)


def solution(mesh):
    in_specs = (
        P("batch", "rows", None, None),
        P("batch", "rows", None, None),
        P(None, "batch"),
        P(),
        P(None, "batch"),
        P(None, "batch"),
        P(),
        P(None, "batch"),
    )
    out_specs = (
        P("batch", "rows", None, None),
        P(None, "batch"),
        P(None, "batch"),
        P(None, "batch"),
        P(None, "batch"),
    )
    return jax.shard_map(local, mesh=mesh, in_specs=in_specs, out_specs=out_specs, check_vma=False)
```

profile of v0, /device:TPU:0, one launch (start us, length us, event | category | flops | bytes accessed | tf_op | source)
XLA Modules:
  0.0 503.2 jit_solution(2143227279648112509)
XLA Ops:
  9.2 5.5 %collective-permute-start = (bf16[1,1,64,384]{3,2,1,0:T(8,128)(2,1)}, bf16[1,1,64,384]{3,2,1,0:T(8,128)(2,1)}, u32[]{:S(2)}, u32[]{:S(2)}) collective-permute-start(bf16[1,1,64,384]{3,2,1,0:T(8,128)(2,1)} %get-tuple-element.53), channel_id=1, source_target_pairs={{0,1},{2,3},{4,5},{6,7},{8,9},{10,11},{12,13},{14,15},{16,17},{18,... | collective-permute-start | bytes 147464 | tf_op jit(solution)/shard_map/ppermute | solution.py:26
  16.9 33.2 %psum.98 = f32[384]{0:T(512)S(1)} all-reduce(f32[384]{0:T(512)S(1)} %reduce_sum.108), channel_id=1, replica_groups=mesh['batch'=16,'rows'=2] {'batch'}, use_global_device_ids=true, to_apply=%region_1.0 | all-reduce | flops 384 | bytes 3072 | tf_op jit(solution)/shard_map/psum | solution.py:67
  51.9 30.0 %all-reduce.5 = (f32[384]{0:T(512)S(1)}, f32[768]{0:T(1024)S(1)}) all-reduce(f32[384]{0:T(512)S(1)} %multiply_reduce_fusion.3, f32[768]{0:T(1024)S(1)} %reduce_sum.110), channel_id=1, replica_groups=mesh['batch'=16,'rows'=2] {'batch'}, use_global_device_ids=true, to_apply=%region_3.0 | all-reduce | flops 1152 | bytes 9216 | tf_op jit(solution)/shard_map/psum | solution.py:78
  84.1 20.0 %all_gather.6 = bf16[384,1152]{0,1:T(8,128)(2,1)S(1)} all-gather(bf16[384,72]{0,1:T(8,128)(2,1)S(1)} %multiply_convert_fusion), channel_id=1, replica_groups=mesh['batch'=16,'rows'=2] {'batch'}, dimensions={1}, use_global_device_ids=true | all-gather | bytes 940032 | tf_op jit(solution)/shard_map/all_gather | solution.py:86
  105.6 1.7 copy.132
  107.3 1.7 copy.133
  116.5 2.1 reshape_squeeze.54
  118.5 1.8 pad_maximum_fusion.2
  120.3 2.0 reshape_squeeze.55
  122.4 2.0 reshape_squeeze.56
  126.3 1.4 reshape_squeeze.61
  127.9 1.4 fusion.74
  134.0 1.5 convolution_bitcast_fusion
  135.6 58.1 %reduce-scatter.5.cloned.1.call-done = f32[768,24]{0,1:T(8,128)} async-done(((f32[768,384]{0,1:T(8,128)}), f32[768,24]{0,1:T(8,128)}) %reduce-scatter.5.cloned.1.call-update) | async-done | bytes 73744 | tf_op jit(solution)/shard_map/reduce_scatter | solution.py:137
  194.8 21.1 %all-reduce.11.cloned.1.call-done = f32[768,24]{0,1:T(8,128)} async-done(((f32[768,24]{0,1:T(8,128)}), f32[768,24]{0,1:T(8,128)}) %all-reduce.11.cloned.1.call-update) | async-done | bytes 73744 | tf_op jit(solution)/shard_map/psum | solution.py:139
  216.0 1.5 multiply_reduce_fusion.7
  217.5 32.9 %psum.101 = f32[768]{0:T(1024)S(1)} all-reduce(f32[768]{0:T(1024)S(1)} %get-tuple-element.9), channel_id=1, replica_groups=mesh['batch'=16,'rows'=2] {'batch'}, use_global_device_ids=true, to_apply=%region_7.0 | all-reduce | flops 768 | bytes 6144 | tf_op jit(solution)/shard_map/psum | solution.py:78
  250.4 18.9 %all_gather.7 = bf16[768,384]{0,1:T(8,128)(2,1)S(1)} all-gather(bf16[768,24]{0,1:T(8,128)(2,1)S(1)} %multiply_convert_fusion.1), channel_id=1, replica_groups=mesh['batch'=16,'rows'=2] {'batch'}, dimensions={1}, use_global_device_ids=true | all-gather | bytes 626688 | tf_op jit(solution)/shard_map/all_gather | solution.py:87
  269.3 2.0 fusion.2
  271.6 2.1 fusion.11
  273.8 2.0 fusion.10
  282.1 3.0 collective-permute-start.2
  287.3 2.8 copy.121
  292.5 1.6 pad_maximum_fusion
  297.9 2.1 reshape_squeeze.65
  300.0 2.0 reshape_squeeze.66
  303.8 2.1 reshape_squeeze.70
  311.4 40.2 %reduce-scatter.7.cloned.1.call-done = f32[384,72]{0,1:T(8,128)} async-done(((f32[384,1152]{0,1:T(8,128)}), f32[384,72]{0,1:T(8,128)}) %reduce-scatter.7.cloned.1.call-update) | async-done | bytes 110608
  352.9 21.0 %all-reduce.9.cloned.1.call-done = f32[384,72]{0,1:T(8,128)} async-done(((f32[384,72]{0,1:T(8,128)}), f32[384,72]{0,1:T(8,128)}) %all-reduce.9.cloned.1.call-update) | async-done | bytes 110608 | tf_op jit(solution)/shard_map/psum | solution.py:139
  374.9 60.8 %all-reduce.4 = (f32[384]{0:T(512)S(1)}, f32[384]{0:T(512)S(1)}, f32[768]{0:T(1024)S(1)}, f32[768]{0:T(1024)S(1)}) all-reduce(f32[384]{0:T(512)S(1)} %get-tuple-element.6, f32[384]{0:T(512)S(1)} %get-tuple-element.7, f32[768]{0:T(1024)S(1)} %copy-done.46, f32[768]{0:T(1024)S(1)} %copy-done.47), channel_id=1, replica_groups=mesh['batch'=16,'rows'=2] {'batch'}, use_global_device_ids=true, to_apply=%region_13.14 | all-reduce | flops 2304 | bytes 18432 | tf_op jit(solution)/shard_map/psum | solution.py:147
  436.7 57.6 %all-reduce.3 = (f32[384]{0:T(512)S(1)}, f32[384]{0:T(512)S(1)}, f32[768]{0:T(1024)S(1)}, f32[768]{0:T(1024)S(1)}) all-reduce(f32[384]{0:T(512)S(1)} %multiply_reduce_fusion, f32[384]{0:T(512)S(1)} %get-tuple-element.5, f32[768]{0:T(1024)S(1)} %multiply_reduce_fusion.5, ...), channel_id=1, replica_groups=mesh['batch'=16,'rows'=2] {'batch'}, use_global_device_ids=true, to_apply=%region_17.18 | all-reduce | flops 2304 | bytes 18432 | tf_op jit(solution)/shard_map/psum | solution.py:154
  495.1 1.6 multiply_subtract_fusion
  (189 shorter events, 50.9 us)
Async XLA Ops:
  7.2 126.8 %copy-start = (bf16[1,8,64,768]{3,2,1,0:T(8,128)(2,1)S(1)}, bf16[1,8,64,768]{3,2,1,0:T(8,128)(2,1)}, u32[]{:S(2)}) copy-start(bf16[1,8,64,768]{3,2,1,0:T(8,128)(2,1)} %param.9) | copy-start | bytes 2359300
  7.2 186.6 %reduce-scatter.5.cloned.1.call-start = ((), (), s32[]{:S(2)}) async-start(), calls=%async_computation.3 | async-start | bytes 1253376 | tf_op jit(solution)/shard_map/reduce_scatter | solution.py:137
  9.2 105.1 %collective-permute-start = (bf16[1,1,64,384]{3,2,1,0:T(8,128)(2,1)}, bf16[1,1,64,384]{3,2,1,0:T(8,128)(2,1)}, u32[]{:S(2)}, u32[]{:S(2)}) collective-permute-start(bf16[1,1,64,384]{3,2,1,0:T(8,128)(2,1)} %get-tuple-element.53), channel_id=1, source_target_pairs={{0,1},{2,3},{4,5},{6,7},{8,9},{10,11},{12,13},{14,15},{16,17},{18,... | collective-permute-start | bytes 147464 | tf_op jit(solution)/shard_map/ppermute | solution.py:26
  14.7 99.6 %collective-permute-start.1 = (bf16[1,1,64,384]{3,2,1,0:T(8,128)(2,1)}, bf16[1,1,64,384]{3,2,1,0:T(8,128)(2,1)}, u32[]{:S(2)}, u32[]{:S(2)}) collective-permute-start(bf16[1,1,64,384]{3,2,1,0:T(8,128)(2,1)} %get-tuple-element.54), channel_id=1, source_target_pairs={{1,0},{3,2},{5,4},{7,6},{9,8},{11,10},{13,12},{15,14},{17,16},{19,... | collective-permute-start | bytes 147464 | tf_op jit(solution)/shard_map/ppermute | solution.py:28
  127.8 5.1 %copy-start.4 = (bf16[512,3,128]{2,1,0:T(4,128)(2,1)}, bf16[512,3,128]{2,1,0:T(4,128)(2,1)S(1)}, u32[]{:S(2)}) copy-start(bf16[512,3,128]{2,1,0:T(4,128)(2,1)S(1)} %reshape_squeeze.61) | copy-start | bytes 1179652
  134.0 135.4 %copy-start.12 = (f32[3,128,512]{2,1,0:T(8,128)}, f32[3,128,512]{2,1,0:T(8,128)S(1)}, u32[]{:S(2)}) copy-start(f32[3,128,512]{2,1,0:T(8,128)S(1)} %get-tuple-element.56) | copy-start | bytes 2359300
  135.5 80.5 %copy-start.13 = (f32[768,24]{0,1:T(8,128)S(1)}, f32[768,24]{0,1:T(8,128)}, u32[]{:S(2)}) copy-start(f32[768,24]{0,1:T(8,128)} %param.13) | copy-start | bytes 221188
  135.5 114.9 %copy-start.43 = (f32[768]{0:T(1024)S(1)}, f32[768]{0:T(1024)}, u32[]{:S(2)}) copy-start(f32[768]{0:T(1024)} %param.14) | copy-start | bytes 9220
  135.5 80.4 %all-reduce.11.cloned.1.call-start = ((), (), s32[]{:S(2)}) async-start(), calls=%async_computation.4 | async-start | bytes 147456 | tf_op jit(solution)/shard_map/psum | solution.py:139
  193.8 157.9 %reduce-scatter.7.cloned.1.call-start = ((), (), s32[]{:S(2)}) async-start(), calls=%async_computation.5 | async-start | bytes 1880064
  271.6 9.9 %copy-start.1 = (bf16[512,384]{1,0:T(8,128)(2,1)}, bf16[512,384]{1,0:T(8,128)(2,1)S(1)}, u32[]{:S(2)}) copy-start(bf16[512,384]{1,0:T(8,128)(2,1)S(1)} %copy.92) | copy-start | bytes 1179652
  271.6 4.2 copy-start.11
  271.6 5.1 %copy-start.9 = (bf16[512,3,128]{2,1,0:T(4,128)(2,1)S(1)}, bf16[512,3,128]{2,1,0:T(4,128)(2,1)}, u32[]{:S(2)}) copy-start(bf16[512,3,128]{2,1,0:T(4,128)(2,1)} %reshape_squeeze.57) | copy-start | bytes 1179652
  273.8 4.9 copy-start.7
  276.8 3.8 copy-start.5
  282.1 9.6 %collective-permute-start.2 = (bf16[1,1,64,384]{3,2,1,0:T(8,128)(2,1)}, bf16[1,1,64,384]{3,2,1,0:T(8,128)(2,1)}, u32[]{:S(2)}, u32[]{:S(2)}) collective-permute-start(bf16[1,1,64,384]{3,2,1,0:T(8,128)(2,1)} %get-tuple-element.49), channel_id=1, source_target_pairs={{0,1},{2,3},{4,5},{6,7},{8,9},{10,11},{12,13},{14,15},{16,17},{18,... | collective-permute-start | bytes 147464 | tf_op jit(solution)/shard_map/ppermute | solution.py:26
  285.1 6.7 %collective-permute-start.3 = (bf16[1,1,64,384]{3,2,1,0:T(8,128)(2,1)}, bf16[1,1,64,384]{3,2,1,0:T(8,128)(2,1)}, u32[]{:S(2)}, u32[]{:S(2)}) collective-permute-start(bf16[1,1,64,384]{3,2,1,0:T(8,128)(2,1)} %get-tuple-element.50), channel_id=1, source_target_pairs={{1,0},{3,2},{5,4},{7,6},{9,8},{11,10},{13,12},{15,14},{17,16},{19,... | collective-permute-start | bytes 147464 | tf_op jit(solution)/shard_map/ppermute | solution.py:28
  291.6 82.3 %all-reduce.9.cloned.1.call-start = ((), (), s32[]{:S(2)}) async-start(), calls=%async_computation.2 | async-start | bytes 221184 | tf_op jit(solution)/shard_map/psum | solution.py:139
  302.0 4.0 copy-start.37
  310.4 41.2 %copy-start.20 = (bf16[1,8,64,384]{3,2,1,0:T(8,128)(2,1)S(1)}, bf16[1,8,64,384]{3,2,1,0:T(8,128)(2,1)}, u32[]{:S(2)}) copy-start(bf16[1,8,64,384]{3,2,1,0:T(8,128)(2,1)} %param.8) | copy-start | bytes 1179652
  310.8 63.1 %copy-start.3 = (f32[384,72]{0,1:T(8,128)S(1)}, f32[384,72]{0,1:T(8,128)}, u32[]{:S(2)}) copy-start(f32[384,72]{0,1:T(8,128)} %param.10) | copy-start | bytes 331780
  310.9 64.0 %copy-start.46 = (f32[768]{0:T(1024)S(1)}, f32[768]{0:T(1024)}, u32[]{:S(2)}) copy-start(f32[768]{0:T(1024)} %get-tuple-element.8) | copy-start | bytes 9220
  310.9 64.0 %copy-start.47 = (f32[768]{0:T(1024)S(1)}, f32[768]{0:T(1024)}, u32[]{:S(2)}) copy-start(f32[768]{0:T(1024)} %get-tuple-element.11) | copy-start | bytes 9220
  310.9 124.7 %copy-start.44 = (f32[768]{0:T(1024)S(1)}, f32[768]{0:T(1024)}, u32[]{:S(2)}) copy-start(f32[768]{0:T(1024)} %param.14) | copy-start | bytes 9220
  310.9 124.7 %copy-start.48 = (f32[384]{0:T(512)S(1)}, f32[384]{0:T(512)}, u32[]{:S(2)}) copy-start(f32[384]{0:T(512)} %param.11) | copy-start | bytes 4612
  310.9 124.7 %copy-start.50 = (f32[384]{0:T(512)S(1)}, f32[384]{0:T(512)}, u32[]{:S(2)}) copy-start(f32[384]{0:T(512)} %copy-done.49) | copy-start | bytes 4612
  310.9 124.8 %copy-start.14 = (f32[768,24]{0,1:T(8,128)S(1)}, f32[768,24]{0,1:T(8,128)}, u32[]{:S(2)}) copy-start(f32[768,24]{0,1:T(8,128)} %param.13) | copy-start | bytes 221188
  310.9 124.8 %copy-start.38 = (f32[768,24]{0,1:T(8,128)S(1)}, f32[768,24]{0,1:T(8,128)}, u32[]{:S(2)}) copy-start(f32[768,24]{0,1:T(8,128)} %all-reduce.11.cloned.1.call-done) | copy-start | bytes 221188
  310.9 124.8 %copy-start.42 = (f32[384]{0:T(512)S(1)}, f32[384]{0:T(512)}, u32[]{:S(2)}) copy-start(f32[384]{0:T(512)} %copy-done.41) | copy-start | bytes 4612
  310.9 125.7 %copy-start.45 = (f32[768]{0:T(1024)S(1)}, f32[768]{0:T(1024)}, u32[]{:S(2)}) copy-start(f32[768]{0:T(1024)} %get-tuple-element.10) | copy-start | bytes 9220
  310.9 183.4 %copy-start.40 = (f32[768,24]{0,1:T(8,128)S(1)}, f32[768,24]{0,1:T(8,128)}, u32[]{:S(2)}) copy-start(f32[768,24]{0,1:T(8,128)} %param.15) | copy-start | bytes 221188
  311.4 183.7 %copy-start.39 = (f32[384,72]{0,1:T(8,128)S(1)}, f32[384,72]{0,1:T(8,128)}, u32[]{:S(2)}) copy-start(f32[384,72]{0,1:T(8,128)} %param.12) | copy-start | bytes 331780
  (27 other events, 35.7 us)
Sparse Core Ops, SparseCore 0:
  135.7 58.0 reduce-scatter.4
  196.0 19.9 all-reduce.10
  291.7 59.9 reduce-scatter.6
  353.8 20.0 all-reduce.8
where the time goes:
time: 505 us; the launch traced here: 503 us
  blocking collectives  253 us (50%)
  waiting for transfers between devices  141 us (28%)
  local copies, waits for them, and re-layouts  42.3 us (8%)
  matrix products  22 us (4%)
  other arithmetic  19.2 us (4%)
  between operations  14.5 us (3%)
  starting transfers between devices  11.3 us (2%)
    psum x2, blocking collectives, local(): lax.psum((jnp.sum(conv_cent * conv_cent, axis=1), jnp.sum(proj_cent * pro...  62.9 us
    psum x1, blocking collectives, local(): row_totals = lax.psum((conv_sum, conv_proj, proj_sum, proj_proj), 'batch')  60.8 us
    reduce_scatter x1, waiting for transfers between devices, local(): lax.psum_scatter(proj_part, 'batch', scatter_dimension=1, tiled=True)  58.1 us
    psum x1, blocking collectives, local(): lax.psum((jnp.sum(conv_raw * conv_raw, axis=1), jnp.sum(proj_raw * proj_r...  57.6 us
    psum x2, waiting for transfers between devices, local(): conv_grad, proj_grad = lax.psum((shares[0], shares[1]), 'rows')  42.1 us
    unnamed x5, waiting for transfers between devices  40.3 us
    psum x1, blocking collectives, local(): lax.psum((jnp.sum(conv_weight, axis=1), jnp.sum(conv_weight * conv_weight...  33.2 us
    all_gather x1, blocking collectives, local(): lax.all_gather(conv_std, 'batch', axis=1, tiled=True)  20 us
  transfers between devices with their start and end apart: 8, of which 4 were waited for; matrix products, arithmetic and copies ran while one was open for 8% of the time, Pallas kernels for 0%

commit v1 on v0

v1 whole, which is shorter than its diff:
```python
import functools
import math

import jax
import jax.numpy as jnp
from jax import lax
from jax.experimental import pallas as pl
from jax.experimental.pallas import tpu as pltpu
from jax.sharding import PartitionSpec as P

ws_eps = 0.0001
clip_ratio = 0.05
momentum_rate = 0.9
learn_rate = 1.6
norm_eps = 1e-06

F32 = jnp.float32
BF16 = jnp.bfloat16
MESH = pl.DeviceIdType.MESH
TAPS = 3
C0 = math.sqrt(2.0 / math.pi)
C1 = 0.044715


def gelu_parts(x):
    t = jnp.tanh(C0 * (x + C1 * (x * x * x)))
    half = 0.5 * (1.0 + t)
    slope = half + (0.5 * C0) * x * (1.0 - t * t) * (1.0 + (3.0 * C1) * (x * x))
    return x * half, slope


def dot_nn(a, b):
    return jnp.dot(a, b, preferred_element_type=F32)


def dot_nt(a, b):
    return lax.dot_general(a, b, (((1,), (1,)), ((), ())), preferred_element_type=F32)


def dot_tn(a, b):
    return lax.dot_general(a, b, (((0,), (0,)), ((), ())), preferred_element_type=F32)


def row_blocks(nc, np_, nblk):
    return [(0, nc)] + [(nc + b * np_, np_) for b in range(nblk)]


def bit_of(me, k):
    return (me // 2**k) % 2


def partner_of(me, k):
    return me + (1 - 2 * bit_of(me, k)) * 2**k


def greet(n):
    me = lax.axis_index("batch")
    r = lax.axis_index("rows")
    barrier = pltpu.get_barrier_semaphore()
    for d in range(1, n):
        pl.semaphore_signal(
            barrier, inc=1, device_id={"batch": (me + d) % n}, device_id_type=MESH
        )
    pl.semaphore_signal(barrier, inc=1, device_id={"rows": 1 - r}, device_id_type=MESH)
    pl.semaphore_wait(barrier, n)


def push_all(n, me, src, slots, send, recv):
    copies = []
    for d in range(1, n):
        copy = pltpu.make_async_remote_copy(
            src_ref=src,
            dst_ref=slots.at[me],
            send_sem=send.at[d - 1],
            recv_sem=recv.at[d - 1],
            device_id={"batch": (me + d) % n},
            device_id_type=MESH,
        )
        copy.start()
        copies.append(copy)
    slots[me] = src[...]
    for copy in copies:
        copy.wait()


def merged(n, slots, at, at_sq, counts, fan):
    total = slots[0, at : at + 1]
    for i in range(1, n):
        total = total + slots[i, at : at + 1]
    mean = total / fan
    spread = None
    for i in range(n):
        off = slots[i, at : at + 1] / counts - mean
        term = slots[i, at_sq : at_sq + 1] + counts * (off * off)
        spread = term if spread is None else spread + term
    return total, mean, spread


def gather_kernel(n, nb, blocks, edge_x, edge_u, w_ref, gain_ref, x_ref, u_ref,
                  full_ref, stat_ref, hx_ref, hu_ref,
                  src, slots, s_send, s_recv, g_send, g_recv, h_send, h_recv):
    me = lax.axis_index("batch")
    r = lax.axis_index("rows")
    greet(n)
    halos = []
    for at, (ref, out, width) in enumerate(((x_ref, hx_ref, edge_x), (u_ref, hu_ref, edge_u))):
        first = (1 - r) * (ref.shape[0] - width)
        copy = pltpu.make_async_remote_copy(
            src_ref=ref.at[pl.ds(first, width)],
            dst_ref=out,
            send_sem=h_send.at[at],
            recv_sem=h_recv.at[at],
            device_id={"rows": 1 - r},
            device_id_type=MESH,
        )
        copy.start()
        halos.append(copy)
    w = w_ref[...]
    src[...] = jnp.zeros_like(src)
    kinds = len(blocks)
    for b, (first, count) in enumerate(blocks):
        piece = w[first : first + count]
        s = jnp.sum(piece, axis=0, keepdims=True)
        cent = piece - s / count
        src[b : b + 1] = s
        src[kinds + b : kinds + b + 1] = jnp.sum(cent * cent, axis=0, keepdims=True)
    push_all(n, me, src, slots, s_send, s_recv)
    pos = 0
    for k in range(nb):
        pos = pos + bit_of(me, k) * 2 ** (nb - 1 - k)
    stat_ref[...] = jnp.zeros_like(stat_ref)
    for b, (first, count) in enumerate(blocks):
        _, mean, spread = merged(n, slots, b, kinds + b, count, n * count)
        stat_ref[b : b + 1] = mean
        stat_ref[kinds + b : kinds + b + 1] = spread
        scale = gain_ref[b : b + 1] * lax.rsqrt(spread + ws_eps)
        full_ref[pos, first : first + count] = (scale * (w[first : first + count] - mean)).astype(BF16)
    for step in range(nb):
        k = nb - 1 - step
        size = 2**step
        base = (pos // size) * size
        copy = pltpu.make_async_remote_copy(
            src_ref=full_ref.at[pl.ds(base, size)],
            dst_ref=full_ref.at[pl.ds(base, size)],
            send_sem=g_send.at[step],
            recv_sem=g_recv.at[step],
            device_id={"batch": partner_of(me, k)},
            device_id_type=MESH,
        )
        copy.start()
        copy.wait()
    for copy in halos:
        copy.wait()


def reduce_kernel(n, nb, images, blocks, part_ref, w_ref, m_ref, stat_ref, gain_ref,
                  new_w_ref, new_m_ref, *scratch):
    recvs = scratch[:nb]
    accs = scratch[nb : 2 * nb]
    recv_x, src, slots, r_send, r_recv, s_send, s_recv, x_send, x_recv = scratch[2 * nb :]
    me = lax.axis_index("batch")
    r = lax.axis_index("rows")
    greet(n)
    cur = part_ref
    for k in range(nb):
        h = n >> (k + 1)
        bit = bit_of(me, k)
        copy = pltpu.make_async_remote_copy(
            src_ref=cur.at[pl.ds((1 - bit) * h, h)],
            dst_ref=recvs[k],
            send_sem=r_send.at[k],
            recv_sem=r_recv.at[k],
            device_id={"batch": partner_of(me, k)},
            device_id_type=MESH,
        )
        copy.start()
        copy.wait()
        acc = accs[k]

        def add(i, carry, cur=cur, acc=acc, rec=recvs[k], first=bit * h):
            acc[i] = (cur[first + i].astype(F32) + rec[i].astype(F32)).astype(acc.dtype)
            return carry

        lax.fori_loop(0, h, add, 0)
        cur = acc
    copy = pltpu.make_async_remote_copy(
        src_ref=cur, dst_ref=recv_x, send_sem=x_send, recv_sem=x_recv,
        device_id={"rows": 1 - r}, device_id_type=MESH,
    )
    copy.start()
    copy.wait()
    grad = (cur[0] + recv_x[0]) / images
    w = w_ref[...]
    kinds = len(blocks)
    src[...] = jnp.zeros_like(src)
    for b, (first, count) in enumerate(blocks):
        piece = grad[first : first + count]
        cent = w[first : first + count] - stat_ref[b : b + 1]
        s = jnp.sum(piece, axis=0, keepdims=True)
        off = piece - s / count
        src[b : b + 1] = s
        src[kinds + b : kinds + b + 1] = jnp.sum(off * off, axis=0, keepdims=True)
        src[2 * kinds + b : 2 * kinds + b + 1] = jnp.sum(piece * cent, axis=0, keepdims=True)
    push_all(n, me, src, slots, s_send, s_recv)
    for b, (first, count) in enumerate(blocks):
        fan = n * count
        _, gmean, gspread = merged(n, slots, b, kinds + b, count, fan)
        at = 2 * kinds + b
        proj = slots[0, at : at + 1]
        for i in range(1, n):
            proj = proj + slots[i, at : at + 1]
        mean = stat_ref[b : b + 1]
        spread = stat_ref[kinds + b : kinds + b + 1]
        factor = lax.rsqrt(spread + ws_eps)
        f2 = factor * factor
        one = gain_ref[b : b + 1] * factor
        two = one * f2 * proj
        grad_sq = one * one * jnp.maximum(gspread - f2 * proj * proj * (2.0 - f2 * spread), 0.0)
        weight_sq = spread + fan * (mean * mean)
        clip = jnp.minimum(1.0, clip_ratio * jnp.sqrt(weight_sq) * lax.rsqrt(grad_sq + norm_eps))
        wp = w[first : first + count]
        raw = one * (grad[first : first + count] - gmean) - two * (wp - mean)
        clipped = clip * raw
        new_m = momentum_rate * m_ref[first : first + count] + clipped
        new_m_ref[first : first + count] = new_m
        new_w_ref[first : first + count] = wp - learn_rate * (clipped + momentum_rate * new_m)


def shifted(vals, step, mc):
    rows = vals.shape[0]
    col = lax.broadcasted_iota(jnp.int32, vals.shape, 0)
    if step > 0:
        return jnp.where(col == mc - 1, 0.0, pltpu.roll(vals, rows - 1, 0))
    return jnp.where(col == 0, 0.0, pltpu.roll(vals, 1, 0))


def compute_kernel(n, order, mr, mc, gw, nc, np_, nblk,
                   x_ref, u_ref, hx_ref, hu_ref, full_ref,
                   ig_ref, part_ref,
                   kt, pt, xs, ys, hid, cg, pg):
    ch = x_ref.shape[1]
    groups = ch // gw
    wide = TAPS * gw
    px = mr * mc
    r = lax.axis_index("rows")
    for d in range(n):
        kt[d * nc : (d + 1) * nc] = full_ref[order[d], :nc]
        for b in range(nblk):
            pt[d * np_ : (d + 1) * np_, b * ch : (b + 1) * ch] = full_ref[
                order[d], nc + b * np_ : nc + (b + 1) * np_
            ]

    def place(at, vals):
        act = gelu_parts(vals)[0].astype(BF16).astype(F32)
        for j in range(TAPS):
            moved = act if j == 1 else shifted(act, j - 1, mc)
            moved = moved.astype(BF16)
            for g in range(groups):
                xs[pl.ds(at, mc), g * wide + j * gw : g * wide + (j + 1) * gw] = moved[
                    :, g * gw : (g + 1) * gw
                ]

    for e in range(2):
        edge = hx_ref[e * mc : (e + 1) * mc].astype(F32)
        place(e * mc, jnp.where(r == 1, edge, 0.0))
        place((mr + 2 + e) * mc, jnp.where(r == 0, edge, 0.0))

    def body(row, carry):
        at = pl.multiple_of(row * mc, mc)
        place(pl.multiple_of(at + 2 * mc, mc), x_ref[pl.ds(at, mc)].astype(F32))
        return carry

    lax.fori_loop(0, mr, body, 0)

    def forward(e, up):
        hg = dot_nt(up, pt[...])
        for g in range(groups):
            acc = None
            for i in range(TAPS):
                term = dot_nn(
                    xs[pl.ds(pl.multiple_of((e + i) * mc, mc), up.shape[0]), g * wide : (g + 1) * wide],
                    kt[i * wide : (i + 1) * wide, g * gw : (g + 1) * gw],
                )
                acc = term if acc is None else acc + term
            h, slope = gelu_parts(acc)
            hid[pl.ds(pl.multiple_of(e * mc, mc), up.shape[0]), g * gw : (g + 1) * gw] = h.astype(BF16)
            grad = (hg[:, g * gw : (g + 1) * gw] * slope).astype(BF16).astype(F32)
            for q in range(up.shape[0] // mc):
                here = grad[q * mc : (q + 1) * mc]
                for j in range(TAPS):
                    moved = here if j == 1 else shifted(here, 1 - j, mc)
                    ys[pl.ds(pl.multiple_of((e + q) * mc, mc), mc), g * wide + j * gw : g * wide + (j + 1) * gw] = moved.astype(BF16)

    edge = hu_ref[...].astype(F32)
    forward(0, jnp.where(r == 1, edge, 0.0).astype(BF16))
    forward(mr + 1, jnp.where(r == 0, edge, 0.0).astype(BF16))
    many = 2 if mr % 2 == 0 else 1

    def fwd(t, carry):
        up = u_ref[pl.ds(pl.multiple_of(t * many * mc, mc), many * mc)]
        forward(1 + t * many, up)
        return carry

    lax.fori_loop(0, mr // many, fwd, 0)

    pg[...] = dot_tn(hid[mc : mc + px], u_ref[...])
    for g in range(groups):
        own = ys[mc : mc + px, g * wide + gw : g * wide + 2 * gw]
        for i in range(TAPS):
            cg[i * wide : (i + 1) * wide, g * gw : (g + 1) * gw] = dot_tn(
                xs[(1 + i) * mc : (1 + i) * mc + px, g * wide : (g + 1) * wide], own
            )
    for d in range(n):
        part_ref[order[d], :nc] = cg[d * nc : (d + 1) * nc].astype(BF16)
        for b in range(nblk):
            part_ref[order[d], nc + b * np_ : nc + (b + 1) * np_] = pg[
                d * np_ : (d + 1) * np_, b * ch : (b + 1) * ch
            ].astype(BF16)

    def back(t, carry):
        at = pl.multiple_of(t * many * mc, mc)
        for g in range(groups):
            acc = None
            for i in range(TAPS):
                for j in range(TAPS):
                    term = dot_nt(
                        ys[pl.ds(pl.multiple_of(at + (2 - i) * mc, mc), many * mc), g * wide + j * gw : g * wide + (j + 1) * gw],
                        kt[i * wide + j * gw : i * wide + (j + 1) * gw, g * gw : (g + 1) * gw],
                    )
                    acc = term if acc is None else acc + term
            slope = gelu_parts(x_ref[pl.ds(at, many * mc), g * gw : (g + 1) * gw].astype(F32))[1]
            ig_ref[pl.ds(at, many * mc), g * gw : (g + 1) * gw] = (acc * slope).astype(BF16)
        return carry

    lax.fori_loop(0, mr // many, back, 0)


def local(n, nrows, block_input, output_grad, conv_weight, conv_gain, conv_momentum,
          proj_weight, proj_gain, proj_momentum):
    assert nrows == 2
    nb = n.bit_length() - 1
    assert 2**nb == n
    _, mr, mc, ch = block_input.shape
    out = output_grad.shape[3]
    nc = conv_weight.shape[1]
    np_ = proj_weight.shape[1]
    nblk = out // ch
    gw = nc * n // (TAPS * TAPS)
    rows = nc + nblk * np_
    blocks = row_blocks(nc, np_, nblk)
    kinds = len(blocks)
    order = [int(format(d, "0%db" % nb)[::-1], 2) for d in range(n)]
    px = mr * mc

    def packed(conv, proj):
        return jnp.concatenate(
            [conv.T] + [proj[b * ch : (b + 1) * ch].T for b in range(nblk)], axis=0
        )

    def unpacked(both):
        conv = both[:nc].T
        proj = jnp.concatenate(
            [both[nc + b * np_ : nc + (b + 1) * np_].T for b in range(nblk)], axis=0
        )
        return conv, proj

    w = packed(conv_weight, proj_weight)
    m = packed(conv_momentum, proj_momentum)
    gain = jnp.concatenate([conv_gain[None], proj_gain.reshape(nblk, ch)], axis=0)
    x = block_input.reshape(px, ch)
    u = output_grad.reshape(px, out)
    vmem = pl.BlockSpec(memory_space=pltpu.VMEM)
    sdt = jax.ShapeDtypeStruct
    stat_rows = -(-2 * kinds // 8) * 8
    grad_rows = -(-3 * kinds // 8) * 8
    dma = pltpu.SemaphoreType.DMA
    full, stat, hx, hu = pl.pallas_call(
        functools.partial(gather_kernel, n, nb, blocks, 2 * mc, mc),
        out_shape=(
            sdt((n, rows, ch), BF16),
            sdt((stat_rows, ch), F32),
            sdt((2 * mc, ch), BF16),
            sdt((mc, out), BF16),
        ),
        in_specs=[vmem] * 4,
        out_specs=(vmem,) * 4,
        scratch_shapes=[
            pltpu.VMEM((stat_rows, ch), F32),
            pltpu.VMEM((n, stat_rows, ch), F32),
            dma((n - 1,)), dma((n - 1,)),
            dma((nb,)), dma((nb,)),
            dma((2,)), dma((2,)),
        ],
        compiler_params=pltpu.CompilerParams(collective_id=0, has_side_effects=True),
        name="gather",
    )(w, gain, x, u)
    ig, part = pl.pallas_call(
        functools.partial(compute_kernel, n, order, mr, mc, gw, nc, np_, nblk),
        out_shape=(sdt((px, ch), BF16), sdt((n, rows, ch), BF16)),
        in_specs=[vmem] * 5,
        out_specs=(vmem,) * 2,
        scratch_shapes=[
            pltpu.VMEM((n * nc, ch), BF16),
            pltpu.VMEM((n * np_, out), BF16),
            pltpu.VMEM(((mr + 4) * mc, TAPS * ch), BF16),
            pltpu.VMEM(((mr + 2) * mc, TAPS * ch), BF16),
            pltpu.VMEM(((mr + 2) * mc, ch), BF16),
            pltpu.VMEM((n * nc, ch), F32),
            pltpu.VMEM((n * np_, out), F32),
        ],
        name="compute",
    )(x, u, hx, hu, full)
    halves = [n >> (k + 1) for k in range(nb)]
    new_w, new_m = pl.pallas_call(
        functools.partial(reduce_kernel, n, nb, n, blocks),
        out_shape=(sdt((rows, ch), F32), sdt((rows, ch), F32)),
        in_specs=[vmem] * 5,
        out_specs=(vmem,) * 2,
        scratch_shapes=[pltpu.VMEM((h, rows, ch), BF16) for h in halves]
        + [pltpu.VMEM((h, rows, ch), BF16 if h > 1 else F32) for h in halves]
        + [
            pltpu.VMEM((1, rows, ch), F32),
            pltpu.VMEM((grad_rows, ch), F32),
            pltpu.VMEM((n, grad_rows, ch), F32),
            dma((nb,)), dma((nb,)),
            dma((n - 1,)), dma((n - 1,)),
            dma, dma,
        ],
        compiler_params=pltpu.CompilerParams(collective_id=1, has_side_effects=True),
        name="reduce",
    )(part, w, m, stat, gain)
    new_conv_w, new_proj_w = unpacked(new_w)
    new_conv_m, new_proj_m = unpacked(new_m)
    return (ig.reshape(block_input.shape), new_conv_w, new_conv_m, new_proj_w, new_proj_m)


def solution(mesh):
    in_specs = (
        P("batch", "rows", None, None),
        P("batch", "rows", None, None),
        P(None, "batch"),
        P(),
        P(None, "batch"),
        P(None, "batch"),
        P(),
        P(None, "batch"),
    )
    out_specs = (
        P("batch", "rows", None, None),
        P(None, "batch"),
        P(None, "batch"),
        P(None, "batch"),
        P(None, "batch"),
    )
    body = functools.partial(local, mesh.shape["batch"], mesh.shape["rows"])
    return jax.shard_map(body, mesh=mesh, in_specs=in_specs, out_specs=out_specs, check_vma=False)
```

time: 505 us -> 98.3 us (0.19)
  blocking collectives: 253 us -> 0 us
  waiting for transfers between devices: 141 us -> 0 us
  Pallas kernels: 0 us -> 88.3 us
  local copies, waits for them, and re-layouts: 42.3 us -> 4.67 us
  matrix products: 22 us -> 0 us
  other arithmetic: 19.2 us -> 4.17 us
  between operations: 14.5 us -> 0.68 us
  starting transfers between devices: 11.3 us -> 0 us
    psum x5 -> x0, blocking collectives: 214 us -> none  [the longest x2 62.9 us: local(): lax.psum((jnp.sum(conv_cent * conv_cent, axis=1), jnp.sum(proj_cent * pro...]
    pallas_call x0 -> x3, Pallas kernels: none -> 88.3 us  [the longest x1 41.3 us: local(): pl.pallas_call(functools.partial(reduce_kernel, n, nb, n, blocks), out_sh...]
    reduce_scatter x1 -> x0, waiting for transfers between devices: 58.1 us -> none  [local(): lax.psum_scatter(proj_part, 'batch', scatter_dimension=1, tiled=True)]
    psum x2 -> x0, waiting for transfers between devices: 42.1 us -> none  [local(): conv_grad, proj_grad = lax.psum((shares[0], shares[1]), 'rows')]
    unnamed x5 -> x0, waiting for transfers between devices: 40.3 us -> none
    all_gather x2 -> x0, blocking collectives: 38.9 us -> none  [the longest x1 20 us: local(): lax.all_gather(conv_std, 'batch', axis=1, tiled=True)]
    another operation x18 -> x0, local copies, waits for them, and re-layouts: 22.1 us -> none  [the longest x9 9.69 us: local(): act_pad[0, top:top + map_rows, left:left + map_cols]]
    dot_general x29 -> x0, matrix products: 22 us -> none  [the longest x9 10.8 us: local(): jnp.einsum('pgi,pgo->goi', patch, grad_groups, preferred_element_type=jnp...]
  transfers between devices with their start and end apart: 8 -> 0, of which waited for: 4 -> 0; matrix products, arithmetic and copies ran while one was open for 8% -> 0% of each run, Pallas kernels for 0% -> 0%
where the time goes in v1:
time: 98.3 us; the launch traced here: 97.8 us
  Pallas kernels  88.3 us (90%)
  local copies, waits for them, and re-layouts  4.67 us (5%)
  other arithmetic  4.17 us (4%)
    pallas_call x1, Pallas kernels, local(): pl.pallas_call(functools.partial(reduce_kernel, n, nb, n, blocks), out_sh...  41.3 us
    pallas_call x1, Pallas kernels, local(): pl.pallas_call(functools.partial(gather_kernel, n, nb, blocks, 2 * mc, mc...  36 us
    pallas_call x1, Pallas kernels, local(): pl.pallas_call(functools.partial(compute_kernel, n, order, mr, mc, gw, nc...  11 us
    concatenate x2, other arithmetic, packed(): jnp.concatenate([conv.T] + [proj[b * ch:(b + 1) * ch].T for b in range(nb...  2.29 us

profile of v1, /device:TPU:0, one launch (start us, length us, event | category | flops | bytes accessed | tf_op | source)
XLA Modules:
  0.0 97.8 jit_solution(17056433961476297954)
XLA Ops:
  0.6 0.8 slice_bitcast_fusion.9
  1.4 1.6 %pad_maximum_fusion.w_ref = f32[120,384]{1,0:T(8,128)} fusion(f32[24,384]{1,0:T(8,128)S(1)} %get-tuple-element.28, f32[24,384]{1,0:T(8,128)S(1)} %get-tuple-element.27, f32[72,384]{1,0:T(8,128)} %bitcast.29), kind=kLoop, calls=%fused_computation | loop fusion | flops 92160 | bytes 368640 | tf_op jit(solution)/shard_map/concatenate | solution.py:356
  3.0 0.7 reshape.24
  3.7 0.7 broadcast_in_dim.3
  4.4 0.6 pad_maximum_fusion.4.gain_ref
  5.0 36.0 %gather.1 = (bf16[16,120,384]{2,1,0:T(8,128)(2,1)}, f32[8,384]{1,0:T(8,128)}, bf16[128,384]{1,0:T(8,128)(2,1)}, bf16[64,768]{1,0:T(8,128)(2,1)}) custom-call(f32[120,384]{1,0:T(8,128)} %pad_maximum_fusion.w_ref, f32[3,384]{1,0:T(4,128)} %pad_maximum_fusion.4.gain_ref, bf16[512,384]{1,0:T(8,128)(2,1)} %bitcast.27, bf16[512,768]{1,0:T(8,128)(2,1)} %bitcast.25), custom_call_target="tpu_custom_call" | custom-call | tf_op jit(solution)/shard_map/gather/pallas_call | solution.py:377
  41.0 0.0 copy-start.1
  41.0 0.0 copy-start
  41.0 11.0 %compute.1 = (bf16[512,384]{1,0:T(8,128)(2,1)}, bf16[16,120,384]{2,1,0:T(8,128)(2,1)}) custom-call(bf16[512,384]{1,0:T(8,128)(2,1)} %bitcast.28, bf16[512,768]{1,0:T(8,128)(2,1)} %bitcast.26, bf16[128,384]{1,0:T(8,128)(2,1)} %get-tuple-element.13.hx_ref, bf16[64,768]{1,0:T(8,128)(2,1)} %get-tuple-element.14.hu_ref, ...), custom_call_target="tpu_custom_call" | custom-call | tf_op jit(solution)/shard_map/compute/pallas_call | solution.py:397
  52.0 0.0 copy-done.1
  52.0 0.0 copy-done
  52.0 0.7 pad_maximum_fusion.1.m_ref
  52.8 41.3 %reduce.1 = (f32[120,384]{1,0:T(8,128)}, f32[120,384]{1,0:T(8,128)}) custom-call(bf16[16,120,384]{2,1,0:T(8,128)(2,1)} %get-tuple-element.17.part_ref, f32[120,384]{1,0:T(8,128)} %pad_maximum_fusion.w_ref, f32[120,384]{1,0:T(8,128)} %pad_maximum_fusion.1.m_ref, f32[8,384]{1,0:T(8,128)} %get-tuple-element.18.stat_ref, f32[3,384]{1,0:T(4,128)} %pad_maximum_fusion.4.gain_ref), custom_call_target="tpu_custom_call" | custom-call | tf_op jit(solution)/shard_map/reduce/pallas_call | solution.py:414
  94.1 0.8 slice_bitcast_fusion.3
  94.9 0.6 pad_maximum_fusion.3
  95.5 0.6 pad_maximum_fusion.2
  96.2 1.6 %slice_bitcast_fusion = (f32[384,72]{0,1:T(8,128)}, f32[384,72]{0,1:T(8,128)}) fusion(f32[120,384]{1,0:T(8,128)} %get-tuple-element.20, f32[120,384]{1,0:T(8,128)} %get-tuple-element.19), kind=kLoop, calls=%fused_computation.2 | loop fusion | bytes 442368 | tf_op jit(solution)/shard_map/transpose | solution.py:361
  (1 shorter events, 0.0 us)
Async XLA Ops:
  41.0 11.1 %copy-start.1 = (f32[768,24]{0,1:T(8,128)S(1)}, f32[768,24]{0,1:T(8,128)}, u32[]{:S(2)}) copy-start(f32[768,24]{0,1:T(8,128)} %param.15) | copy-start | bytes 221188
  41.0 11.1 %copy-start = (f32[384,72]{0,1:T(8,128)S(1)}, f32[384,72]{0,1:T(8,128)}, u32[]{:S(2)}) copy-start(f32[384,72]{0,1:T(8,128)} %param.12) | copy-start | bytes 331780

commit v2 on v1

--- a/solution.py
+++ b/solution.py
@@ -41,10 +41,6 @@
     return lax.dot_general(a, b, (((0,), (0,)), ((), ())), preferred_element_type=F32)
 
 
-def row_blocks(nc, np_, nblk):
-    return [(0, nc)] + [(nc + b * np_, np_) for b in range(nblk)]
-
-
 def bit_of(me, k):
     return (me // 2**k) % 2
 
@@ -53,7 +49,7 @@
     return me + (1 - 2 * bit_of(me, k)) * 2**k
 
 
-def greet(n):
+def greet_signal(n):
     me = lax.axis_index("batch")
     r = lax.axis_index("rows")
     barrier = pltpu.get_barrier_semaphore()
@@ -62,10 +58,13 @@
             barrier, inc=1, device_id={"batch": (me + d) % n}, device_id_type=MESH
         )
     pl.semaphore_signal(barrier, inc=1, device_id={"rows": 1 - r}, device_id_type=MESH)
-    pl.semaphore_wait(barrier, n)
-
-
-def push_all(n, me, src, slots, send, recv):
+
+
+def greet_wait(n):
+    pl.semaphore_wait(pltpu.get_barrier_semaphore(), n)
+
+
+def push_start(n, me, src, slots, send, recv):
     copies = []
     for d in range(1, n):
         copy = pltpu.make_async_remote_copy(
@@ -79,8 +78,7 @@
         copy.start()
         copies.append(copy)
     slots[me] = src[...]
-    for copy in copies:
-        copy.wait()
+    return copies
 
 
 def merged(n, slots, at, at_sq, counts, fan):
@@ -96,12 +94,33 @@
     return total, mean, spread
 
 
-def gather_kernel(n, nb, blocks, edge_x, edge_u, w_ref, gain_ref, x_ref, u_ref,
+LANE = 128
+
+
+def kind_slices(ch, out):
+    return [(0, 0)] + [(1, b * ch) for b in range(out // ch)]
+
+
+def gather_kernel(n, nb, pieces, edge_x, edge_u, wc_ref, wp_ref, gc_ref, gp_ref, x_ref, u_ref,
                   full_ref, stat_ref, hx_ref, hu_ref,
                   src, slots, s_send, s_recv, g_send, g_recv, h_send, h_recv):
     me = lax.axis_index("batch")
     r = lax.axis_index("rows")
-    greet(n)
+    greet_signal(n)
+    ch = wc_ref.shape[1]
+    kinds = kind_slices(ch, wp_ref.shape[1])
+    nk = len(kinds)
+    w_refs = (wc_ref, wp_ref)
+    gain_refs = (gc_ref, gp_ref)
+    src[...] = jnp.zeros_like(src)
+    for b, (which, col) in enumerate(kinds):
+        piece = w_refs[which][:, col : col + ch]
+        s = jnp.sum(piece, axis=0, keepdims=True)
+        cent = piece - s / piece.shape[0]
+        src[b : b + 1] = s
+        src[nk + b : nk + b + 1] = jnp.sum(cent * cent, axis=0, keepdims=True)
+    greet_wait(n)
+    push = push_start(n, me, src, slots, s_send, s_recv)
     halos = []
     for at, (ref, out, width) in enumerate(((x_ref, hx_ref, edge_x), (u_ref, hu_ref, edge_u))):
         first = (1 - r) * (ref.shape[0] - width)
@@ -115,115 +134,145 @@
         )
         copy.start()
         halos.append(copy)
-    w = w_ref[...]
-    src[...] = jnp.zeros_like(src)
-    kinds = len(blocks)
-    for b, (first, count) in enumerate(blocks):
-        piece = w[first : first + count]
-        s = jnp.sum(piece, axis=0, keepdims=True)
-        cent = piece - s / count
-        src[b : b + 1] = s
-        src[kinds + b : kinds + b + 1] = jnp.sum(cent * cent, axis=0, keepdims=True)
-    push_all(n, me, src, slots, s_send, s_recv)
+    for copy in push:
+        copy.wait()
     pos = 0
     for k in range(nb):
         pos = pos + bit_of(me, k) * 2 ** (nb - 1 - k)
     stat_ref[...] = jnp.zeros_like(stat_ref)
-    for b, (first, count) in enumerate(blocks):
-        _, mean, spread = merged(n, slots, b, kinds + b, count, n * count)
+    first = 0
+    for b, (which, col) in enumerate(kinds):
+        count = w_refs[which].shape[0]
+        _, mean, spread = merged(n, slots, b, nk + b, count, n * count)
         stat_ref[b : b + 1] = mean
-        stat_ref[kinds + b : kinds + b + 1] = spread
-        scale = gain_ref[b : b + 1] * lax.rsqrt(spread + ws_eps)
-        full_ref[pos, first : first + count] = (scale * (w[first : first + count] - mean)).astype(BF16)
-    for step in range(nb):
-        k = nb - 1 - step
-        size = 2**step
-        base = (pos // size) * size
-        copy = pltpu.make_async_remote_copy(
-            src_ref=full_ref.at[pl.ds(base, size)],
-            dst_ref=full_ref.at[pl.ds(base, size)],
-            send_sem=g_send.at[step],
-            recv_sem=g_recv.at[step],
-            device_id={"batch": partner_of(me, k)},
-            device_id_type=MESH,
-        )
-        copy.start()
-        copy.wait()
+        stat_ref[nk + b : nk + b + 1] = spread
+        scale = gain_refs[which][:, col : col + ch] * lax.rsqrt(spread + ws_eps)
+        std = (scale * (w_refs[which][:, col : col + ch] - mean)).astype(BF16)
+        for p in range(pieces):
+            full_ref[p, pos, first : first + count] = std[:, p * LANE : (p + 1) * LANE]
+        first += count
+    flight = [None] * pieces
+    for t in range(nb + pieces):
+        for p in range(pieces):
+            step = t - p
+            if step < 0 or step > nb:
+                continue
+            if flight[p] is not None:
+                flight[p].wait()
+            if step == nb:
+                continue
+            size = 2**step
+            base = (pos // size) * size
+            flight[p] = pltpu.make_async_remote_copy(
+                src_ref=full_ref.at[p, pl.ds(base, size)],
+                dst_ref=full_ref.at[p, pl.ds(base, size)],
+                send_sem=g_send.at[p, step],
+                recv_sem=g_recv.at[p, step],
+                device_id={"batch": partner_of(me, nb - 1 - step)},
+                device_id_type=MESH,
+            )
+            flight[p].start()
     for copy in halos:
         copy.wait()
 
 
-def reduce_kernel(n, nb, images, blocks, part_ref, w_ref, m_ref, stat_ref, gain_ref,
-                  new_w_ref, new_m_ref, *scratch):
+def reduce_kernel(n, nb, pieces, images, part_ref, wc_ref, wp_ref, mc_ref, mp_ref, stat_ref,
+                  gc_ref, gp_ref, nwc_ref, nwp_ref, nmc_ref, nmp_ref, *scratch):
     recvs = scratch[:nb]
     accs = scratch[nb : 2 * nb]
     recv_x, src, slots, r_send, r_recv, s_send, s_recv, x_send, x_recv = scratch[2 * nb :]
     me = lax.axis_index("batch")
     r = lax.axis_index("rows")
-    greet(n)
-    cur = part_ref
-    for k in range(nb):
-        h = n >> (k + 1)
-        bit = bit_of(me, k)
-        copy = pltpu.make_async_remote_copy(
-            src_ref=cur.at[pl.ds((1 - bit) * h, h)],
-            dst_ref=recvs[k],
-            send_sem=r_send.at[k],
-            recv_sem=r_recv.at[k],
-            device_id={"batch": partner_of(me, k)},
-            device_id_type=MESH,
-        )
-        copy.start()
-        copy.wait()
-        acc = accs[k]
-
-        def add(i, carry, cur=cur, acc=acc, rec=recvs[k], first=bit * h):
-            acc[i] = (cur[first + i].astype(F32) + rec[i].astype(F32)).astype(acc.dtype)
-            return carry
-
-        lax.fori_loop(0, h, add, 0)
-        cur = acc
-    copy = pltpu.make_async_remote_copy(
-        src_ref=cur, dst_ref=recv_x, send_sem=x_send, recv_sem=x_recv,
-        device_id={"rows": 1 - r}, device_id_type=MESH,
-    )
-    copy.start()
-    copy.wait()
-    grad = (cur[0] + recv_x[0]) / images
-    w = w_ref[...]
-    kinds = len(blocks)
+    greet_signal(n)
+    greet_wait(n)
+    flight = [None] * pieces
+    for t in range(nb + 1 + pieces):
+        for p in range(pieces):
+            k = t - p
+            if k < 0 or k > nb + 1:
+                continue
+            if flight[p] is not None:
+                flight[p].wait()
+            if 1 <= k <= nb:
+                h = n >> k
+                cur = part_ref if k == 1 else accs[k - 2]
+                acc = accs[k - 1]
+                rec = recvs[k - 1]
+                lo = bit_of(me, k - 1) * h
+
+                def add(i, carry, cur=cur, acc=acc, rec=rec, lo=lo, p=p):
+                    acc[p, i] = (cur[p, lo + i].astype(F32) + rec[p, i].astype(F32)).astype(acc.dtype)
+                    return carry
+
+                lax.fori_loop(0, h, add, 0)
+            if k < nb:
+                h = n >> (k + 1)
+                cur = part_ref if k == 0 else accs[k - 1]
+                flight[p] = pltpu.make_async_remote_copy(
+                    src_ref=cur.at[p, pl.ds((1 - bit_of(me, k)) * h, h)],
+                    dst_ref=recvs[k].at[p],
+                    send_sem=r_send.at[p, k],
+                    recv_sem=r_recv.at[p, k],
+                    device_id={"batch": partner_of(me, k)},
+                    device_id_type=MESH,
+                )
+                flight[p].start()
+            elif k == nb:
+                flight[p] = pltpu.make_async_remote_copy(
+                    src_ref=accs[nb - 1].at[p],
+                    dst_ref=recv_x.at[p],
+                    send_sem=x_send.at[p],
+                    recv_sem=x_recv.at[p],
+                    device_id={"rows": 1 - r},
+                    device_id_type=MESH,
+                )
+                flight[p].start()
+    last = accs[nb - 1]
+    grad = jnp.concatenate([last[p, 0] + recv_x[p, 0] for p in range(pieces)], axis=1) / images
+    ch = wc_ref.shape[1]
+    kinds = kind_slices(ch, wp_ref.shape[1])
+    nk = len(kinds)
+    w_refs = (wc_ref, wp_ref)
+    gain_refs = (gc_ref, gp_ref)
     src[...] = jnp.zeros_like(src)
-    for b, (first, count) in enumerate(blocks):
+    parts = []
+    first = 0
+    for b, (which, col) in enumerate(kinds):
+        count = w_refs[which].shape[0]
         piece = grad[first : first + count]
-        cent = w[first : first + count] - stat_ref[b : b + 1]
+        parts.append(piece)
+        first += count
+        cent = w_refs[which][:, col : col + ch] - stat_ref[b : b + 1]
         s = jnp.sum(piece, axis=0, keepdims=True)
         off = piece - s / count
         src[b : b + 1] = s
-        src[kinds + b : kinds + b + 1] = jnp.sum(off * off, axis=0, keepdims=True)
-        src[2 * kinds + b : 2 * kinds + b + 1] = jnp.sum(piece * cent, axis=0, keepdims=True)
-    push_all(n, me, src, slots, s_send, s_recv)
-    for b, (first, count) in enumerate(blocks):
+        src[nk + b : nk + b + 1] = jnp.sum(off * off, axis=0, keepdims=True)
+        src[2 * nk + b : 2 * nk + b + 1] = jnp.sum(piece * cent, axis=0, keepdims=True)
+    for copy in push_start(n, me, src, slots, s_send, s_recv):
+        copy.wait()
+    for b, (which, col) in enumerate(kinds):
+        count = w_refs[which].shape[0]
+        cols = slice(col, col + ch)
         fan = n * count
-        _, gmean, gspread = merged(n, slots, b, kinds + b, count, fan)
-        at = 2 * kinds + b
+        _, gmean, gspread = merged(n, slots, b, nk + b, count, fan)
+        at = 2 * nk + b
         proj = slots[0, at : at + 1]
         for i in range(1, n):
             proj = proj + slots[i, at : at + 1]
         mean = stat_ref[b : b + 1]
-        spread = stat_ref[kinds + b : kinds + b + 1]
+        spread = stat_ref[nk + b : nk + b + 1]
         factor = lax.rsqrt(spread + ws_eps)
         f2 = factor * factor
-        one = gain_ref[b : b + 1] * factor
+        one = gain_refs[which][:, cols] * factor
         two = one * f2 * proj
         grad_sq = one * one * jnp.maximum(gspread - f2 * proj * proj * (2.0 - f2 * spread), 0.0)
         weight_sq = spread + fan * (mean * mean)
         clip = jnp.minimum(1.0, clip_ratio * jnp.sqrt(weight_sq) * lax.rsqrt(grad_sq + norm_eps))
-        wp = w[first : first + count]
-        raw = one * (grad[first : first + count] - gmean) - two * (wp - mean)
-        clipped = clip * raw
-        new_m = momentum_rate * m_ref[first : first + count] + clipped
-        new_m_ref[first : first + count] = new_m
-        new_w_ref[first : first + count] = wp - learn_rate * (clipped + momentum_rate * new_m)
+        wp = w_refs[which][:, cols]
+        clipped = clip * (one * (parts[b] - gmean) - two * (wp - mean))
+        new_m = momentum_rate * (mc_ref, mp_ref)[which][:, cols] + clipped
+        (nmc_ref, nmp_ref)[which][:, cols] = new_m
+        (nwc_ref, nwp_ref)[which][:, cols] = wp - learn_rate * (clipped + momentum_rate * new_m)
 
 
 def shifted(vals, step, mc):
@@ -244,11 +293,13 @@
     px = mr * mc
     r = lax.axis_index("rows")
     for d in range(n):
-        kt[d * nc : (d + 1) * nc] = full_ref[order[d], :nc]
-        for b in range(nblk):
-            pt[d * np_ : (d + 1) * np_, b * ch : (b + 1) * ch] = full_ref[
-                order[d], nc + b * np_ : nc + (b + 1) * np_
-            ]
+        for p in range(ch // LANE):
+            kt[d * nc : (d + 1) * nc, p * LANE : (p + 1) * LANE] = full_ref[p, order[d], :nc]
+            for b in range(nblk):
+                at = b * ch + p * LANE
+                pt[d * np_ : (d + 1) * np_, at : at + LANE] = full_ref[
+                    p, order[d], nc + b * np_ : nc + (b + 1) * np_
+                ]
 
     def place(at, vals):
         act = gelu_parts(vals)[0].astype(BF16).astype(F32)
@@ -311,11 +362,15 @@
                 xs[(1 + i) * mc : (1 + i) * mc + px, g * wide : (g + 1) * wide], own
             )
     for d in range(n):
-        part_ref[order[d], :nc] = cg[d * nc : (d + 1) * nc].astype(BF16)
-        for b in range(nblk):
-            part_ref[order[d], nc + b * np_ : nc + (b + 1) * np_] = pg[
-                d * np_ : (d + 1) * np_, b * ch : (b + 1) * ch
+        for p in range(ch // LANE):
+            part_ref[p, order[d], :nc] = cg[
+                d * nc : (d + 1) * nc, p * LANE : (p + 1) * LANE
             ].astype(BF16)
+            for b in range(nblk):
+                at = b * ch + p * LANE
+                part_ref[p, order[d], nc + b * np_ : nc + (b + 1) * np_] = pg[
+                    d * np_ : (d + 1) * np_, at : at + LANE
+                ].astype(BF16)
 
     def back(t, carry):
         at = pl.multiple_of(t * many * mc, mc)
@@ -347,26 +402,13 @@
     nblk = out // ch
     gw = nc * n // (TAPS * TAPS)
     rows = nc + nblk * np_
-    blocks = row_blocks(nc, np_, nblk)
-    kinds = len(blocks)
+    kinds = 1 + nblk
+    pieces = ch // LANE
     order = [int(format(d, "0%db" % nb)[::-1], 2) for d in range(n)]
     px = mr * mc
 
-    def packed(conv, proj):
-        return jnp.concatenate(
-            [conv.T] + [proj[b * ch : (b + 1) * ch].T for b in range(nblk)], axis=0
-        )
-
-    def unpacked(both):
-        conv = both[:nc].T
-        proj = jnp.concatenate(
-            [both[nc + b * np_ : nc + (b + 1) * np_].T for b in range(nblk)], axis=0
-        )
-        return conv, proj
-
-    w = packed(conv_weight, proj_weight)
-    m = packed(conv_momentum, proj_momentum)
-    gain = jnp.concatenate([conv_gain[None], proj_gain.reshape(nblk, ch)], axis=0)
+    wc, wp, mc_, mp = conv_weight.T, proj_weight.T, conv_momentum.T, proj_momentum.T
+    gc, gp = conv_gain[None], proj_gain[None]
     x = block_input.reshape(px, ch)
     u = output_grad.reshape(px, out)
     vmem = pl.BlockSpec(memory_space=pltpu.VMEM)
@@ -375,28 +417,28 @@
     grad_rows = -(-3 * kinds // 8) * 8
     dma = pltpu.SemaphoreType.DMA
     full, stat, hx, hu = pl.pallas_call(
-        functools.partial(gather_kernel, n, nb, blocks, 2 * mc, mc),
+        functools.partial(gather_kernel, n, nb, pieces, 2 * mc, mc),
         out_shape=(
-            sdt((n, rows, ch), BF16),
+            sdt((pieces, n, rows, LANE), BF16),
             sdt((stat_rows, ch), F32),
             sdt((2 * mc, ch), BF16),
             sdt((mc, out), BF16),
         ),
-        in_specs=[vmem] * 4,
+        in_specs=[vmem] * 6,
         out_specs=(vmem,) * 4,
         scratch_shapes=[
             pltpu.VMEM((stat_rows, ch), F32),
             pltpu.VMEM((n, stat_rows, ch), F32),
             dma((n - 1,)), dma((n - 1,)),
-            dma((nb,)), dma((nb,)),
+            dma((pieces, nb)), dma((pieces, nb)),
             dma((2,)), dma((2,)),
         ],
         compiler_params=pltpu.CompilerParams(collective_id=0, has_side_effects=True),
         name="gather",
-    )(w, gain, x, u)
+    )(wc, wp, gc, gp, x, u)
     ig, part = pl.pallas_call(
         functools.partial(compute_kernel, n, order, mr, mc, gw, nc, np_, nblk),
-        out_shape=(sdt((px, ch), BF16), sdt((n, rows, ch), BF16)),
+        out_shape=(sdt((px, ch), BF16), sdt((pieces, n, rows, LANE), BF16)),
         in_specs=[vmem] * 5,
         out_specs=(vmem,) * 2,
         scratch_shapes=[
@@ -411,27 +453,25 @@
         name="compute",
     )(x, u, hx, hu, full)
     halves = [n >> (k + 1) for k in range(nb)]
-    new_w, new_m = pl.pallas_call(
-        functools.partial(reduce_kernel, n, nb, n, blocks),
-        out_shape=(sdt((rows, ch), F32), sdt((rows, ch), F32)),
-        in_specs=[vmem] * 5,
-        out_specs=(vmem,) * 2,
-        scratch_shapes=[pltpu.VMEM((h, rows, ch), BF16) for h in halves]
-        + [pltpu.VMEM((h, rows, ch), BF16 if h > 1 else F32) for h in halves]
+    nwc, nwp, nmc, nmp = pl.pallas_call(
+        functools.partial(reduce_kernel, n, nb, pieces, n),
+        out_shape=(sdt((nc, ch), F32), sdt((np_, out), F32)) * 2,
+        in_specs=[vmem] * 8,
+        out_specs=(vmem,) * 4,
+        scratch_shapes=[pltpu.VMEM((pieces, h, rows, LANE), BF16) for h in halves]
+        + [pltpu.VMEM((pieces, h, rows, LANE), BF16 if h > 1 else F32) for h in halves]
         + [
-            pltpu.VMEM((1, rows, ch), F32),
+            pltpu.VMEM((pieces, 1, rows, LANE), F32),
             pltpu.VMEM((grad_rows, ch), F32),
             pltpu.VMEM((n, grad_rows, ch), F32),
-            dma((nb,)), dma((nb,)),
+            dma((pieces, nb)), dma((pieces, nb)),
             dma((n - 1,)), dma((n - 1,)),
-            dma, dma,
+            dma((pieces,)), dma((pieces,)),
         ],
         compiler_params=pltpu.CompilerParams(collective_id=1, has_side_effects=True),
         name="reduce",
-    )(part, w, m, stat, gain)
-    new_conv_w, new_proj_w = unpacked(new_w)
-    new_conv_m, new_proj_m = unpacked(new_m)
-    return (ig.reshape(block_input.shape), new_conv_w, new_conv_m, new_proj_w, new_proj_m)
+    )(part, wc, wp, mc_, mp, stat, gc, gp)
+    return (ig.reshape(block_input.shape), nwc.T, nmc.T, nwp.T, nmp.T)
 
 
 def solution(mesh):

time: 98.3 us -> 92.1 us (0.937)
  Pallas kernels: 88.3 us -> 82.4 us
  other arithmetic: 4.17 us -> 0 us
  local copies, waits for them, and re-layouts: 4.67 us -> 8.65 us
    unnamed x4, local copies, waits for them, and re-layouts: 0.01 us -> 6.14 us
    pallas_call x2, Pallas kernels: 77.3 us -> 71.2 us  [the longest x1 35.9 us: local(): pl.pallas_call(functools.partial(gather_kernel, n, nb, pieces, 2 * mc, mc...]
    concatenate x5 -> x0, other arithmetic: 4.17 us -> none  [the longest x2 2.29 us: packed(): jnp.concatenate([conv.T] + [proj[b * ch:(b + 1) * ch].T for b in range(nb...]
    transpose x4 -> x0, local copies, waits for them, and re-layouts: 3.28 us -> none  [the longest x1 1.65 us: unpacked(): conv = both[:nc].T]
    broadcast_in_dim x1 -> x2, local copies, waits for them, and re-layouts: 0.68 us -> 2.51 us  [local(): gc, gp = (conv_gain[None], proj_gain[None])]
where the time goes in v2:
time: 92.1 us; the launch traced here: 91.7 us
  Pallas kernels  82.4 us (89%)
  local copies, waits for them, and re-layouts  8.65 us (9%)
    pallas_call x1, Pallas kernels, local(): pl.pallas_call(functools.partial(gather_kernel, n, nb, pieces, 2 * mc, mc...  35.9 us
    pallas_call x1, Pallas kernels, local(): pl.pallas_call(functools.partial(reduce_kernel, n, nb, pieces, n), out_sh...  35.3 us
    pallas_call x1, Pallas kernels, local(): pl.pallas_call(functools.partial(compute_kernel, n, order, mr, mc, gw, nc...  11.1 us
    unnamed x4, local copies, waits for them, and re-layouts  6.14 us
    broadcast_in_dim x2, local copies, waits for them, and re-layouts, local(): gc, gp = (conv_gain[None], proj_gain[None])  2.51 us

profile of v2, /device:TPU:0, one launch (start us, length us, event | category | flops | bytes accessed | tf_op | source)
XLA Modules:
  0.0 91.7 jit_solution(17591344161826051473)
XLA Ops:
  0.6 1.2 %broadcast_in_dim.6.gc_ref = f32[1,384]{1,0:T(1,128)} reshape(f32[384]{0:T(512)} %param.11) | data formatting | bytes 3072 | tf_op jit(solution)/shard_map/broadcast_in_dim | solution.py:411
  1.9 1.3 %broadcast_in_dim.7.gp_ref = f32[1,768]{1,0:T(1,128)} reshape(f32[768]{0:T(1024)} %param.14) | data formatting | bytes 6144 | tf_op jit(solution)/shard_map/broadcast_in_dim | solution.py:411
  3.1 35.9 %gather.1 = (bf16[3,16,120,128]{3,2,1,0:T(8,128)(2,1)}, f32[8,384]{1,0:T(8,128)}, bf16[128,384]{1,0:T(8,128)(2,1)}, bf16[64,768]{1,0:T(8,128)(2,1)}) custom-call(f32[72,384]{1,0:T(8,128)} %bitcast.15, f32[24,768]{1,0:T(8,128)} %bitcast.17, f32[1,384]{1,0:T(1,128)} %broadcast_in_dim.6.gc_ref, f32[1,768]{1,0:T(1,128)} %broadcast_in_dim.7.gp_ref, ...), custom_call_target="tpu_custom_call" | custom-call | tf_op jit(solution)/shard_map/gather/pallas_call | solution.py:419
  39.0 11.1 %compute.1 = (bf16[512,384]{1,0:T(8,128)(2,1)}, bf16[3,16,120,128]{3,2,1,0:T(8,128)(2,1)}) custom-call(bf16[512,384]{1,0:T(8,128)(2,1)} %bitcast.14, bf16[512,768]{1,0:T(8,128)(2,1)} %bitcast.12, bf16[128,384]{1,0:T(8,128)(2,1)} %get-tuple-element.15.hx_ref, bf16[64,768]{1,0:T(8,128)(2,1)} %get-tuple-element.16.hu_ref, ...), custom_call_target="tpu_custom_call" | custom-call | tf_op jit(solution)/shard_map/compute/pallas_call | solution.py:439
  50.2 35.3 %reduce.1 = (f32[72,384]{1,0:T(8,128)}, f32[24,768]{1,0:T(8,128)}, f32[72,384]{1,0:T(8,128)}, f32[24,768]{1,0:T(8,128)}) custom-call(bf16[3,16,120,128]{3,2,1,0:T(8,128)(2,1)} %get-tuple-element.19.part_ref, f32[72,384]{1,0:T(8,128)} %bitcast.16, f32[24,768]{1,0:T(8,128)} %bitcast.18, f32[72,384]{1,0:T(8,128)} %bitcast.21, f32[24,768]{1,0:T(8,128)} %bitcast.22, ...), custom_call_target="tpu_custom_call" | custom-call | tf_op jit(solution)/shard_map/reduce/pallas_call | solution.py:456
  85.5 1.5 %copy.17 = f32[384,72]{0,1:T(8,128)} copy(f32[384,72]{0,1:T(8,128)} %bitcast.20) | data formatting | bytes 221184
  87.1 1.5 %copy.18 = f32[384,72]{0,1:T(8,128)} copy(f32[384,72]{0,1:T(8,128)} %bitcast.19) | data formatting | bytes 221184
  88.6 1.5 %copy.19 = f32[768,24]{0,1:T(8,128)} copy(f32[768,24]{0,1:T(8,128)} %bitcast.24) | data formatting | bytes 147456
  90.1 1.5 %copy.20 = f32[768,24]{0,1:T(8,128)} copy(f32[768,24]{0,1:T(8,128)} %bitcast.23) | data formatting | bytes 147456

commit v3 on v2

--- a/solution.py
+++ b/solution.py
@@ -77,19 +77,20 @@
         )
         copy.start()
         copies.append(copy)
-    slots[me] = src[...]
+    for row in range(src.shape[0]):
+        slots[me, row] = src[row]
     return copies
 
 
 def merged(n, slots, at, at_sq, counts, fan):
-    total = slots[0, at : at + 1]
+    total = slots[0, at]
     for i in range(1, n):
-        total = total + slots[i, at : at + 1]
+        total = total + slots[i, at]
     mean = total / fan
     spread = None
     for i in range(n):
-        off = slots[i, at : at + 1] / counts - mean
-        term = slots[i, at_sq : at_sq + 1] + counts * (off * off)
+        off = slots[i, at] / counts - mean
+        term = slots[i, at_sq] + counts * (off * off)
         spread = term if spread is None else spread + term
     return total, mean, spread
 
@@ -112,13 +113,12 @@
     nk = len(kinds)
     w_refs = (wc_ref, wp_ref)
     gain_refs = (gc_ref, gp_ref)
-    src[...] = jnp.zeros_like(src)
     for b, (which, col) in enumerate(kinds):
         piece = w_refs[which][:, col : col + ch]
         s = jnp.sum(piece, axis=0, keepdims=True)
         cent = piece - s / piece.shape[0]
-        src[b : b + 1] = s
-        src[nk + b : nk + b + 1] = jnp.sum(cent * cent, axis=0, keepdims=True)
+        src[b] = s
+        src[nk + b] = jnp.sum(cent * cent, axis=0, keepdims=True)
     greet_wait(n)
     push = push_start(n, me, src, slots, s_send, s_recv)
     halos = []
@@ -146,7 +146,7 @@
         _, mean, spread = merged(n, slots, b, nk + b, count, n * count)
         stat_ref[b : b + 1] = mean
         stat_ref[nk + b : nk + b + 1] = spread
-        scale = gain_refs[which][:, col : col + ch] * lax.rsqrt(spread + ws_eps)
+        scale = gain_refs[which][col : col + ch][None] * lax.rsqrt(spread + ws_eps)
         std = (scale * (w_refs[which][:, col : col + ch] - mean)).astype(BF16)
         for p in range(pieces):
             full_ref[p, pos, first : first + count] = std[:, p * LANE : (p + 1) * LANE]
@@ -176,8 +176,8 @@
         copy.wait()
 
 
-def reduce_kernel(n, nb, pieces, images, part_ref, wc_ref, wp_ref, mc_ref, mp_ref, stat_ref,
-                  gc_ref, gp_ref, nwc_ref, nwp_ref, nmc_ref, nmp_ref, *scratch):
+def reduce_kernel(n, nb, pieces, images, part_ref, wc_ref, wp_ref, stat_ref,
+                  gc_ref, gp_ref, grad_ref, coef_ref, *scratch):
     recvs = scratch[:nb]
     accs = scratch[nb : 2 * nb]
     recv_x, src, slots, r_send, r_recv, s_send, s_recv, x_send, x_recv = scratch[2 * nb :]
@@ -229,25 +229,24 @@
                 flight[p].start()
     last = accs[nb - 1]
     grad = jnp.concatenate([last[p, 0] + recv_x[p, 0] for p in range(pieces)], axis=1) / images
+    grad_ref[...] = grad
+    coef_ref[...] = jnp.zeros_like(coef_ref)
     ch = wc_ref.shape[1]
     kinds = kind_slices(ch, wp_ref.shape[1])
     nk = len(kinds)
     w_refs = (wc_ref, wp_ref)
     gain_refs = (gc_ref, gp_ref)
-    src[...] = jnp.zeros_like(src)
-    parts = []
     first = 0
     for b, (which, col) in enumerate(kinds):
         count = w_refs[which].shape[0]
         piece = grad[first : first + count]
-        parts.append(piece)
         first += count
         cent = w_refs[which][:, col : col + ch] - stat_ref[b : b + 1]
         s = jnp.sum(piece, axis=0, keepdims=True)
         off = piece - s / count
-        src[b : b + 1] = s
-        src[nk + b : nk + b + 1] = jnp.sum(off * off, axis=0, keepdims=True)
-        src[2 * nk + b : 2 * nk + b + 1] = jnp.sum(piece * cent, axis=0, keepdims=True)
+        src[b] = s
+        src[nk + b] = jnp.sum(off * off, axis=0, keepdims=True)
+        src[2 * nk + b] = jnp.sum(piece * cent, axis=0, keepdims=True)
     for copy in push_start(n, me, src, slots, s_send, s_recv):
         copy.wait()
     for b, (which, col) in enumerate(kinds):
@@ -256,23 +255,42 @@
         fan = n * count
         _, gmean, gspread = merged(n, slots, b, nk + b, count, fan)
         at = 2 * nk + b
-        proj = slots[0, at : at + 1]
+        proj = slots[0, at]
         for i in range(1, n):
-            proj = proj + slots[i, at : at + 1]
+            proj = proj + slots[i, at]
         mean = stat_ref[b : b + 1]
         spread = stat_ref[nk + b : nk + b + 1]
         factor = lax.rsqrt(spread + ws_eps)
         f2 = factor * factor
-        one = gain_refs[which][:, cols] * factor
+        one = gain_refs[which][cols][None] * factor
         two = one * f2 * proj
         grad_sq = one * one * jnp.maximum(gspread - f2 * proj * proj * (2.0 - f2 * spread), 0.0)
         weight_sq = spread + fan * (mean * mean)
         clip = jnp.minimum(1.0, clip_ratio * jnp.sqrt(weight_sq) * lax.rsqrt(grad_sq + norm_eps))
-        wp = w_refs[which][:, cols]
-        clipped = clip * (one * (parts[b] - gmean) - two * (wp - mean))
+        coef_ref[b : b + 1] = clip * one
+        coef_ref[nk + b : nk + b + 1] = gmean
+        coef_ref[2 * nk + b : 2 * nk + b + 1] = clip * two
+
+
+def update_kernel(grad_ref, coef_ref, stat_ref, wc_ref, wp_ref, mc_ref, mp_ref,
+                  nwc_ref, nwp_ref, nmc_ref, nmp_ref):
+    ch = wc_ref.shape[1]
+    kinds = kind_slices(ch, wp_ref.shape[1])
+    nk = len(kinds)
+    first = 0
+    for b, (which, col) in enumerate(kinds):
+        w_ref = (wc_ref, wp_ref)[which]
+        count = w_ref.shape[0]
+        cols = slice(col, col + ch)
+        w = w_ref[:, cols]
+        grad = grad_ref[first : first + count]
+        first += count
+        clipped = coef_ref[b : b + 1] * (grad - coef_ref[nk + b : nk + b + 1]) - coef_ref[
+            2 * nk + b : 2 * nk + b + 1
+        ] * (w - stat_ref[b : b + 1])
         new_m = momentum_rate * (mc_ref, mp_ref)[which][:, cols] + clipped
         (nmc_ref, nmp_ref)[which][:, cols] = new_m
-        (nwc_ref, nwp_ref)[which][:, cols] = wp - learn_rate * (clipped + momentum_rate * new_m)
+        (nwc_ref, nwp_ref)[which][:, cols] = w - learn_rate * (clipped + momentum_rate * new_m)
 
 
 def shifted(vals, step, mc):
@@ -408,7 +426,7 @@
     px = mr * mc
 
     wc, wp, mc_, mp = conv_weight.T, proj_weight.T, conv_momentum.T, proj_momentum.T
-    gc, gp = conv_gain[None], proj_gain[None]
+    gc, gp = conv_gain, proj_gain
     x = block_input.reshape(px, ch)
     u = output_grad.reshape(px, out)
     vmem = pl.BlockSpec(memory_space=pltpu.VMEM)
@@ -427,8 +445,8 @@
         in_specs=[vmem] * 6,
         out_specs=(vmem,) * 4,
         scratch_shapes=[
-            pltpu.VMEM((stat_rows, ch), F32),
-            pltpu.VMEM((n, stat_rows, ch), F32),
+            pltpu.VMEM((2 * kinds, 1, ch), F32),
+            pltpu.VMEM((n, 2 * kinds, 1, ch), F32),
             dma((n - 1,)), dma((n - 1,)),
             dma((pieces, nb)), dma((pieces, nb)),
             dma((2,)), dma((2,)),
@@ -453,24 +471,31 @@
         name="compute",
     )(x, u, hx, hu, full)
     halves = [n >> (k + 1) for k in range(nb)]
-    nwc, nwp, nmc, nmp = pl.pallas_call(
+    grad, coef = pl.pallas_call(
         functools.partial(reduce_kernel, n, nb, pieces, n),
-        out_shape=(sdt((nc, ch), F32), sdt((np_, out), F32)) * 2,
-        in_specs=[vmem] * 8,
-        out_specs=(vmem,) * 4,
+        out_shape=(sdt((rows, ch), F32), sdt((grad_rows, ch), F32)),
+        in_specs=[vmem] * 6,
+        out_specs=(vmem,) * 2,
         scratch_shapes=[pltpu.VMEM((pieces, h, rows, LANE), BF16) for h in halves]
         + [pltpu.VMEM((pieces, h, rows, LANE), BF16 if h > 1 else F32) for h in halves]
         + [
             pltpu.VMEM((pieces, 1, rows, LANE), F32),
-            pltpu.VMEM((grad_rows, ch), F32),
-            pltpu.VMEM((n, grad_rows, ch), F32),
+            pltpu.VMEM((3 * kinds, 1, ch), F32),
+            pltpu.VMEM((n, 3 * kinds, 1, ch), F32),
             dma((pieces, nb)), dma((pieces, nb)),
             dma((n - 1,)), dma((n - 1,)),
             dma((pieces,)), dma((pieces,)),
         ],
         compiler_params=pltpu.CompilerParams(collective_id=1, has_side_effects=True),
         name="reduce",
-    )(part, wc, wp, mc_, mp, stat, gc, gp)
+    )(part, wc, wp, stat, gc, gp)
+    nwc, nwp, nmc, nmp = pl.pallas_call(
+        update_kernel,
+        out_shape=(sdt((nc, ch), F32), sdt((np_, out), F32)) * 2,
+        in_specs=[vmem] * 7,
+        out_specs=(vmem,) * 4,
+        name="update",
+    )(grad, coef, stat, wc, wp, mc_, mp)
     return (ig.reshape(block_input.shape), nwc.T, nmc.T, nwp.T, nmp.T)
 
 

time: 92.1 us -> 83.7 us (0.909)
  local copies, waits for them, and re-layouts: 8.65 us -> 0 us
    unnamed x4 -> x0, local copies, waits for them, and re-layouts: 6.14 us -> none
    broadcast_in_dim x2 -> x0, local copies, waits for them, and re-layouts: 2.51 us -> none  [local(): gc, gp = (conv_gain[None], proj_gain[None])]
    pallas_call x0 -> x1, Pallas kernels: none -> 1.92 us  [local(): pl.pallas_call(update_kernel, out_shape=(sdt((nc, ch), F32), sdt((np_, ou...]
where the time goes in v3:
time: 83.7 us; the launch traced here: 83.4 us
  Pallas kernels  82.8 us (99%)
    pallas_call x1, Pallas kernels, local(): pl.pallas_call(functools.partial(gather_kernel, n, nb, pieces, 2 * mc, mc...  35 us
    pallas_call x1, Pallas kernels, local(): pl.pallas_call(functools.partial(reduce_kernel, n, nb, pieces, n), out_sh...  34.7 us
    pallas_call x1, Pallas kernels, local(): pl.pallas_call(functools.partial(compute_kernel, n, order, mr, mc, gw, nc...  11.1 us
    pallas_call x1, Pallas kernels, local(): pl.pallas_call(update_kernel, out_shape=(sdt((nc, ch), F32), sdt((np_, ou...  1.92 us

profile of v3, /device:TPU:0, one launch (start us, length us, event | category | flops | bytes accessed | tf_op | source)
XLA Modules:
  0.0 83.4 jit_solution(17638194929125096658)
XLA Ops:
  0.6 35.0 %gather.1 = (bf16[3,16,120,128]{3,2,1,0:T(8,128)(2,1)}, f32[8,384]{1,0:T(8,128)}, bf16[128,384]{1,0:T(8,128)(2,1)}, bf16[64,768]{1,0:T(8,128)(2,1)}) custom-call(f32[72,384]{1,0:T(8,128)} %bitcast.15, f32[24,768]{1,0:T(8,128)} %bitcast.18, f32[384]{0:T(512)} %gc_ref.3, f32[768]{0:T(1024)} %gp_ref.3, bf16[512,384]{1,0:T(8,128)(2,1)} %bitcast.13, ...), custom_call_target="tpu_custom_call" | custom-call | tf_op jit(solution)/shard_map/gather/pallas_call | solution.py:437
  35.7 11.1 %compute.1 = (bf16[512,384]{1,0:T(8,128)(2,1)}, bf16[3,16,120,128]{3,2,1,0:T(8,128)(2,1)}) custom-call(bf16[512,384]{1,0:T(8,128)(2,1)} %bitcast.14, bf16[512,768]{1,0:T(8,128)(2,1)} %bitcast.12, bf16[128,384]{1,0:T(8,128)(2,1)} %get-tuple-element.17.hx_ref, bf16[64,768]{1,0:T(8,128)(2,1)} %get-tuple-element.18.hu_ref, ...), custom_call_target="tpu_custom_call" | custom-call | tf_op jit(solution)/shard_map/compute/pallas_call | solution.py:457
  46.8 34.7 %reduce.1 = (f32[120,384]{1,0:T(8,128)}, f32[16,384]{1,0:T(8,128)}) custom-call(bf16[3,16,120,128]{3,2,1,0:T(8,128)(2,1)} %get-tuple-element.21.part_ref, f32[72,384]{1,0:T(8,128)} %bitcast.16, f32[24,768]{1,0:T(8,128)} %bitcast.19, f32[8,384]{1,0:T(8,128)} %get-tuple-element.22.stat_ref, f32[384]{0:T(512)} %gc_ref.3, f32[768]{0:T(1024)} %gp_ref.3), custom_call_target="tpu_custom_call" | custom-call | tf_op jit(solution)/shard_map/reduce/pallas_call | solution.py:474
  81.5 1.9 %update.1 = (f32[72,384]{1,0:T(8,128)}, f32[24,768]{1,0:T(8,128)}, f32[72,384]{1,0:T(8,128)}, f32[24,768]{1,0:T(8,128)}) custom-call(f32[120,384]{1,0:T(8,128)} %get-tuple-element.23.grad_ref, f32[16,384]{1,0:T(8,128)} %get-tuple-element.24.coef_ref, f32[8,384]{1,0:T(8,128)} %get-tuple-element.22.stat_ref, f32[72,384]{1,0:T(8,128)} %bitcast.17, ...), custom_call_target="tpu_custom_call" | custom-call | tf_op jit(solution)/shard_map/update/pallas_call | solution.py:492
